TPU v7x, 32 devices: a whole 2x2x4 slice. The times are simulated.
32 devices in a mesh: grp: 4 (over y, core), seq: 8 (over z, x).
Axes of the slice: x: 2, y: 2, z: 4, core: 2. Of those that a mesh axis runs over, the one named last changes fastest.
Arguments:
- layer_input: bfloat16 [8192, 2048], P(('grp', 'seq')), may hold values from -6 to 6
- entry_gain: float32 [2048], replicated, may hold values from 0.1 to 1.9
- entry_shift: float32 [2048], replicated, may hold values from -1.75 to 1.75
- joint_weight: bfloat16 [2048, 6144], P(('grp', 'seq')), may hold values from -0.125 to 0.125
- query_offset: float32 [2048], replicated, may hold values from -3 to 3
- value_offset: float32 [2048], replicated, may hold values from -0.3125 to 0.3125
- mixing_weight: bfloat16 [2048, 2048], P(('grp', 'seq')), may hold values from -1 to 1
- attention_offset: float32 [2048], replicated, may hold values from -3 to 3
- middle_gain: float32 [2048], replicated, may hold values from 0.1 to 1.9
- middle_shift: float32 [2048], replicated, may hold values from -1.75 to 1.75
- expand_weight: bfloat16 [2048, 8192], P(('grp', 'seq')), may hold values from -0.125 to 0.125
- expand_offset: float32 [8192], replicated, may hold values from -3 to 3
- shrink_weight: bfloat16 [2048, 8192], P(('grp', 'seq')), may hold values from -0.0625 to 0.0625
- shrink_offset: float32 [2048], replicated, may hold values from -3 to 3
- placement: int32 [4, 2048], P('grp'), may hold values from 0 to 2047, each once within a row
- slot_lengths: int32 [4, 4], P('grp'), may hold values from 1 to 256, 832 in all within a row
- cotangent: bfloat16 [8192, 2048], P(('grp', 'seq')), may hold values from -6 to 6
Outputs:
- layer_output: bfloat16 [8192, 2048], P(('grp', 'seq'))
- input_gradient: bfloat16 [8192, 2048], P(('grp', 'seq'))
- entry_gain_gradient: float32 [2048], replicated
- entry_shift_gradient: float32 [2048], replicated
- joint_gradient: float32 [2048, 6144], P(('grp', 'seq'))
- query_gradient: float32 [2048], replicated
- value_gradient: float32 [2048], replicated
- mixing_gradient: float32 [2048, 2048], P(('grp', 'seq'))
- attention_offset_gradient: float32 [2048], replicated
- middle_gain_gradient: float32 [2048], replicated
- middle_shift_gradient: float32 [2048], replicated
- expand_gradient: float32 [2048, 8192], P(('grp', 'seq'))
- expand_offset_gradient: float32 [8192], replicated
- shrink_gradient: float32 [2048, 8192], P(('grp', 'seq'))
- shrink_offset_gradient: float32 [2048], replicated
Inputs may be any that keep to these rules, and one draw needn't show every extreme that they name: `placement`: each row holds every position of its group once. `slot_lengths`: the real tokens of each slot of 256 positions; the rest of a slot is padding; some slot of every group is full.
All inputs are finite; a program needn't handle non-finite values.
Results may differ from a plain program's by a relative error of at most 0.013.
Values may be sent and summed in bfloat16 or wider, within the bound.
A program may use at most 704 MiB of HBM per device.

v0:
```python
import jax
import jax.numpy as jnp
from jax import lax
from jax.sharding import Mesh, PartitionSpec as P

HEADS = 16
CONT = 256
QBLOCK = 512
PLANE = ("grp", "sub")
EVERY = ("grp", "rep", "sub")
norm_epsilon = 1e-05
masked_score = -1e30


def norm_terms(values):
    average = jnp.mean(values, axis=-1, keepdims=True)
    centered = values - average
    variance = jnp.mean(centered * centered, axis=-1, keepdims=True)
    inverse = lax.rsqrt(variance + norm_epsilon)
    return (centered * inverse, inverse)


def norm_back(slope, gain, normal, inverse):
    scaled = slope * gain
    return inverse * (
        scaled
        - jnp.mean(scaled, axis=-1, keepdims=True)
        - normal * jnp.mean(scaled * normal, axis=-1, keepdims=True)
    )


def exact_gelu(values):
    return jax.nn.gelu(values, approximate=False)


def key_bounds(positions, lengths, prompt):
    segment = (positions - prompt) // CONT
    within = positions - prompt - segment * CONT
    slot_ids = jnp.arange(lengths.shape[0], dtype=jnp.int32)
    slot_limit = jnp.sum(
        jnp.where(segment[:, None] == slot_ids[None, :], lengths[None, :], 0), axis=1
    )
    last = prompt + (segment + 1) * CONT - 1
    last = jnp.where(within < slot_limit, last, -1)
    return jnp.where(positions < prompt, positions.shape[0], last)


def block_mask(query_place, key_place, key_last):
    query_col = query_place[:, None]
    return (key_place[None, :] <= query_col) & (query_col <= key_last[None, :])


def product(left_matrix, right_matrix):
    return jnp.dot(left_matrix, right_matrix, preferred_element_type=jnp.float32)


def product_transposed(left_matrix, right_matrix):
    return lax.dot_general(
        left_matrix, right_matrix, (((1,), (1,)), ((), ())), preferred_element_type=jnp.float32
    )


def row_outer(left_matrix, right_matrix):
    return lax.dot_general(
        left_matrix, right_matrix, (((0,), (0,)), ((), ())), preferred_element_type=jnp.float32
    )


def attention_forward(grouped, places, key_last, score_scale):
    queries = grouped[:, :, 0]
    key_vectors = grouped[:, :, 1]
    values = grouped[:, :, 2]
    rows_total = grouped.shape[0]

    def one_block(block_index):
        first_row = block_index * QBLOCK
        block_queries = lax.dynamic_slice_in_dim(queries, first_row, QBLOCK, 0)
        block_places = lax.dynamic_slice_in_dim(places, first_row, QBLOCK, 0)
        allowed = block_mask(block_places, places, key_last)
        scores = (
            jnp.einsum(
                "qhe,khe->hqk", block_queries, key_vectors, preferred_element_type=jnp.float32
            )
            * score_scale
        )
        scores = jnp.where(allowed[None], scores, masked_score)
        row_top = jnp.max(scores, axis=2, keepdims=True)
        row_total = jnp.sum(jnp.exp(scores - row_top), axis=2, keepdims=True)
        log_total = row_top + jnp.log(row_total)
        soft_weights = jnp.exp(scores - log_total).astype(jnp.bfloat16)
        mixture = jnp.einsum(
            "hqk,khe->qhe", soft_weights, values, preferred_element_type=jnp.float32
        )
        return (mixture.astype(jnp.bfloat16), jnp.transpose(log_total[:, :, 0]))

    mixture, log_totals = lax.map(one_block, jnp.arange(rows_total // QBLOCK, dtype=jnp.int32))
    return (mixture.reshape(rows_total, -1), log_totals.reshape(rows_total, -1))


def attention_backward(grouped, log_totals, slopes, places, key_last, score_scale):
    queries = grouped[:, :, 0]
    key_vectors = grouped[:, :, 1]
    values = grouped[:, :, 2]
    rows_total = grouped.shape[0]

    def one_block(running, block_index):
        key_sum, value_sum = running
        first_row = block_index * QBLOCK
        block_queries = lax.dynamic_slice_in_dim(queries, first_row, QBLOCK, 0)
        block_slopes = lax.dynamic_slice_in_dim(slopes, first_row, QBLOCK, 0)
        block_totals = lax.dynamic_slice_in_dim(log_totals, first_row, QBLOCK, 0)
        block_places = lax.dynamic_slice_in_dim(places, first_row, QBLOCK, 0)
        allowed = block_mask(block_places, places, key_last)
        scores = (
            jnp.einsum(
                "qhe,khe->hqk", block_queries, key_vectors, preferred_element_type=jnp.float32
            )
            * score_scale
        )
        scores = jnp.where(allowed[None], scores, masked_score)
        probable = jnp.exp(scores - jnp.transpose(block_totals)[:, :, None])
        weight_slope = jnp.einsum(
            "qhe,khe->hqk", block_slopes, values, preferred_element_type=jnp.float32
        )
        centre = jnp.sum(probable * weight_slope, axis=2, keepdims=True)
        score_slope = (probable * (weight_slope - centre)).astype(jnp.bfloat16)
        query_slope = (
            jnp.einsum("hqk,khe->qhe", score_slope, key_vectors, preferred_element_type=jnp.float32)
            * score_scale
        )
        key_sum = (
            key_sum
            + jnp.einsum(
                "hqk,qhe->khe", score_slope, block_queries, preferred_element_type=jnp.float32
            )
            * score_scale
        )
        value_sum = value_sum + jnp.einsum(
            "hqk,qhe->khe",
            probable.astype(jnp.bfloat16),
            block_slopes,
            preferred_element_type=jnp.float32,
        )
        return ((key_sum, value_sum), query_slope)

    empty_sums = jnp.zeros(values.shape, jnp.float32)
    (key_sum, value_sum), query_slopes = lax.scan(
        one_block, (empty_sums, empty_sums), jnp.arange(rows_total // QBLOCK, dtype=jnp.int32)
    )
    query_slopes = query_slopes.reshape(values.shape)
    return jnp.stack([query_slopes, key_sum, value_sum], axis=2).astype(jnp.bfloat16)


def plane_columns(weight, plane_count):
    rows, columns = weight.shape
    own = lax.all_to_all(
        weight.reshape(rows, plane_count, columns // plane_count),
        PLANE,
        split_axis=1,
        concat_axis=0,
        tiled=True,
    ).reshape(plane_count * rows, columns // plane_count)
    every = lax.all_gather(own, "rep", axis=0, tiled=True)
    groups, reps, subs = (lax.axis_size(name) for name in EVERY)
    every = every.reshape(reps, groups, subs, rows, -1).transpose(1, 0, 2, 3, 4)
    return every.reshape(reps * groups * subs * rows, -1)


def owner_rows(gradient, plane_count):
    groups, reps, subs = (lax.axis_size(name) for name in EVERY)
    columns = gradient.shape[1]
    rows = gradient.shape[0] // (groups * reps * subs)
    ordered = gradient.astype(jnp.bfloat16).reshape(groups, reps, subs, rows, columns)
    ordered = ordered.transpose(1, 0, 2, 3, 4).reshape(-1, columns)
    summed = lax.psum_scatter(ordered, "rep", scatter_dimension=0, tiled=True)
    own = lax.all_to_all(
        summed.reshape(plane_count, rows, columns), PLANE, split_axis=0, concat_axis=0, tiled=True
    )
    return own.transpose(1, 0, 2).reshape(rows, plane_count * columns).astype(jnp.float32)


def shards(
    layer_input,
    entry_gain,
    entry_shift,
    joint_weight,
    query_offset,
    value_offset,
    mixing_weight,
    attention_offset,
    middle_gain,
    middle_shift,
    expand_weight,
    expand_offset,
    shrink_weight,
    shrink_offset,
    placement,
    slot_lengths,
    cotangent,
):
    token_rows, width = layer_input.shape
    hidden_width = expand_weight.shape[1]
    groups, reps, subs = (lax.axis_size(name) for name in EVERY)
    plane_count = groups * subs
    plane_index = lax.axis_index(PLANE)
    rep_index = lax.axis_index("rep")
    head_size = width // HEADS
    local_heads = HEADS // plane_count
    head_columns = local_heads * head_size
    score_scale = head_size ** (-0.5)
    placements = lax.all_gather(placement, "grp", axis=0, tiled=True)
    lengths_all = lax.all_gather(slot_lengths, "grp", axis=0, tiled=True)
    places = lax.dynamic_index_in_dim(placements, rep_index, 0, keepdims=False)
    lengths = lax.dynamic_index_in_dim(lengths_all, rep_index, 0, keepdims=False)
    prompt = places.shape[0] // 2
    key_last = key_bounds(places, lengths, prompt)
    joint_slice = plane_columns(joint_weight, plane_count)
    expand_slice = plane_columns(expand_weight, plane_count)
    shrink_slice = plane_columns(shrink_weight, plane_count)
    mixing_whole = lax.all_gather(mixing_weight, EVERY, axis=0, tiled=True)
    input_float = layer_input.astype(jnp.float32)
    entry_normal, entry_inverse = norm_terms(input_float)
    entry_normed = (entry_normal * entry_gain + entry_shift).astype(jnp.bfloat16)
    entry_all = lax.all_gather(entry_normed, PLANE, axis=0, tiled=True)
    plane_rows = entry_all.shape[0]
    offsets = jnp.stack(
        [
            query_offset.reshape(HEADS, head_size),
            jnp.zeros((HEADS, head_size), jnp.float32),
            value_offset.reshape(HEADS, head_size),
        ],
        axis=1,
    ).reshape(-1)
    offsets = lax.dynamic_slice_in_dim(offsets, plane_index * 3 * head_columns, 3 * head_columns)
    joint_values = (product(entry_all, joint_slice) + offsets).astype(jnp.bfloat16)
    heads_kept = lax.all_to_all(
        joint_values.reshape(groups, plane_rows // groups, 3 * head_columns),
        "rep",
        split_axis=0,
        concat_axis=0,
        tiled=True,
    ).reshape(plane_rows, local_heads, 3, head_size)
    mixture, log_totals = attention_forward(heads_kept, places, key_last, score_scale)

    def to_tokens(array):
        columns = array.shape[1]
        at_plane = lax.all_to_all(
            array.reshape(reps, plane_rows // reps, columns),
            "rep",
            split_axis=0,
            concat_axis=0,
            tiled=True,
        )
        return at_plane.reshape(plane_count, token_rows, columns)

    attended = lax.all_to_all(to_tokens(mixture), PLANE, split_axis=0, concat_axis=0, tiled=True)
    attended = attended.transpose(1, 0, 2).reshape(token_rows, width)
    residual = input_float + (product(attended, mixing_whole) + attention_offset)
    middle_normal, middle_inverse = norm_terms(residual)
    middle_normed = (middle_normal * middle_gain + middle_shift).astype(jnp.bfloat16)
    middle_all = lax.all_gather(middle_normed, PLANE, axis=0, tiled=True)
    cotangent_all = lax.all_gather(cotangent, PLANE, axis=0, tiled=True)
    hidden_local = hidden_width // plane_count
    offset_local = lax.dynamic_slice_in_dim(expand_offset, plane_index * hidden_local, hidden_local)
    expanded = product(middle_all, expand_slice) + offset_local
    activated_float, gelu_back = jax.vjp(exact_gelu, expanded)
    activated = activated_float.astype(jnp.bfloat16)
    activated_slope = product(cotangent_all, shrink_slice)
    expanded_slope = gelu_back(activated_slope)[0].astype(jnp.bfloat16)
    slope_part = product_transposed(expanded_slope, expand_slice).astype(jnp.bfloat16)
    normed_slope = lax.psum_scatter(slope_part, PLANE, scatter_dimension=0, tiled=True).astype(
        jnp.float32
    )
    output_part = product_transposed(activated, shrink_slice).astype(jnp.bfloat16)
    shrunk = lax.psum_scatter(output_part, PLANE, scatter_dimension=0, tiled=True)
    layer_output = (residual + shrunk.astype(jnp.float32) + shrink_offset).astype(jnp.bfloat16)
    cotangent_float = cotangent.astype(jnp.float32)
    residual_slope = cotangent_float + norm_back(
        normed_slope, middle_gain, middle_normal, middle_inverse
    )
    branch_slope = residual_slope.astype(jnp.bfloat16)
    attended_slope = product_transposed(branch_slope, mixing_whole).astype(jnp.bfloat16)
    slope_plane = lax.all_to_all(
        attended_slope.reshape(token_rows, plane_count, head_columns).transpose(1, 0, 2),
        PLANE,
        split_axis=0,
        concat_axis=0,
        tiled=True,
    )
    head_slopes = lax.all_to_all(
        slope_plane.reshape(groups, plane_rows // groups, head_columns),
        "rep",
        split_axis=0,
        concat_axis=0,
        tiled=True,
    ).reshape(plane_rows, local_heads, head_size)
    joint_heads = attention_backward(
        heads_kept, log_totals, head_slopes, places, key_last, score_scale
    )
    joint_slope = to_tokens(joint_heads.reshape(plane_rows, 3 * head_columns)).reshape(
        plane_rows, 3 * head_columns
    )
    entry_part = product_transposed(joint_slope, joint_slice).astype(jnp.bfloat16)
    entry_slope = lax.psum_scatter(entry_part, PLANE, scatter_dimension=0, tiled=True).astype(
        jnp.float32
    )
    input_gradient = (
        residual_slope + norm_back(entry_slope, entry_gain, entry_normal, entry_inverse)
    ).astype(jnp.bfloat16)
    slope_sums = jnp.sum(joint_slope.astype(jnp.float32), axis=0).reshape(local_heads, 3, head_size)

    def placed(piece, whole_size):
        return lax.dynamic_update_slice_in_dim(
            jnp.zeros((whole_size,), jnp.float32), piece, plane_index * piece.shape[0], 0
        )

    small_sums = lax.psum(
        (
            jnp.sum(entry_slope * entry_normal, axis=0),
            jnp.sum(entry_slope, axis=0),
            placed(slope_sums[:, 0].reshape(-1), width),
            placed(slope_sums[:, 2].reshape(-1), width),
            jnp.sum(branch_slope.astype(jnp.float32), axis=0),
            jnp.sum(normed_slope * middle_normal, axis=0),
            jnp.sum(normed_slope, axis=0),
            placed(jnp.sum(expanded_slope.astype(jnp.float32), axis=0), hidden_width),
            jnp.sum(cotangent_float, axis=0),
        ),
        EVERY,
    )
    shrink_gradient = owner_rows(row_outer(cotangent_all, activated), plane_count)
    expand_gradient = owner_rows(row_outer(middle_all, expanded_slope), plane_count)
    mixing_gradient = lax.psum_scatter(
        row_outer(attended, branch_slope).astype(jnp.bfloat16),
        EVERY,
        scatter_dimension=0,
        tiled=True,
    ).astype(jnp.float32)
    joint_gradient = owner_rows(row_outer(entry_all, joint_slope), plane_count)
    return (
        layer_output,
        input_gradient,
        small_sums[0],
        small_sums[1],
        joint_gradient,
        small_sums[2],
        small_sums[3],
        mixing_gradient,
        small_sums[4],
        small_sums[5],
        small_sums[6],
        expand_gradient,
        small_sums[7],
        shrink_gradient,
        small_sums[8],
    )


def solution(mesh):
    groups, sequence = (mesh.shape["grp"], mesh.shape["seq"])
    subs = sequence // groups
    planes = Mesh(mesh.devices.reshape(groups, sequence // subs, subs), EVERY)
    rows, whole, group_rows = (P(EVERY, None), P(), P("grp", None))
    return jax.shard_map(
        shards,
        mesh=planes,
        in_specs=(
            rows,
            whole,
            whole,
            rows,
            whole,
            whole,
            rows,
            whole,
            whole,
            whole,
            rows,
            whole,
            rows,
        )
        + (whole, group_rows, group_rows, rows),
        out_specs=(
            rows,
            rows,
            whole,
            whole,
            rows,
            whole,
            whole,
            rows,
            whole,
            whole,
            whole,
            rows,
            whole,
        )
        + (rows, whole),
        check_vma=False,
    )
```

profile of v0, /device:TPU:8, one launch (start us, length us, event | category | flops | bytes accessed | tf_op | source)
XLA Modules:
  0.0 1536.1 jit_solution(3426588837099018649)
XLA Ops:
  8.5 15.8 %all_to_all.90 = bf16[64,8,768]{2,0,1:T(8,128)(2,1)} all-to-all(bf16[64,8,768]{2,0,1:T(8,128)(2,1)S(1)} %bitcast.227), channel_id=1, replica_groups=mesh['grp'=4,'rep'=4,'sub'=2] {'grp','sub'}, dimensions={1} | all-to-all | bytes 1572864 | tf_op jit(solution)/shard_map/all_to_all | solution.py:156
  51.7 33.8 %all-gather.12.cloned.1.call-done = bf16[2048,768]{1,0:T(8,128)(2,1)} async-done(((bf16[512,768]{1,0:T(8,128)(2,1)}), bf16[2048,768]{1,0:T(8,128)(2,1)}) %all-gather.12.cloned.1.call-update) | async-done | bytes 3145744 | tf_op jit(solution)/shard_map/all_gather | solution.py:163
  89.3 54.0 %all-gather.10.cloned.1.call-done = bf16[2048,2048]{1,0:T(8,128)(2,1)} async-done(((bf16[256,2048]{1,0:T(8,128)(2,1)}), bf16[2048,2048]{1,0:T(8,128)(2,1)}) %all-gather.10.cloned.1.call-update) | async-done | bytes 8388624 | tf_op jit(solution)/shard_map/all_gather | solution.py:224
  175.4 90.0 %all-to-all-done.1 = bf16[4,512,768]{1,2,0:T(8,128)(2,1)} async-done(((bf16[4,512,768]{1,2,0:T(8,128)(2,1)}), bf16[4,512,768]{1,2,0:T(8,128)(2,1)}, u32[]{:S(2)}, u32[]{:S(2)}) %all-to-all-start.1) | async-done | bytes 3145760 | tf_op jit(solution)/shard_map/all_to_all | solution.py:236
  284.3 53.2 %while.27 = (s32[]{:T(128)}, bf16[4,512,2,128]{1,3,2,0:T(8,128)(2,1)}, f32[4,512,2]{1,2,0:T(2,128)}, s32[2048]{0:T(1024)S(1)}, s32[4]{0:T(128)S(1)}, /*index=5*/...) while((s32[]{:T(128)}, ...), condition=%wide.region_6.7_spmd, body=%wide.region_3.6_spmd.sunk | while | flops 1100086272 | bytes 33086656 | solution.py:96
  337.5 36.7 %all_to_all.91 = bf16[4,512,256]{1,2,0:T(8,128)(2,1)} all-to-all(bf16[4,512,256]{1,2,0:T(8,128)(2,1)} %bitcast.238), channel_id=1, replica_groups=mesh['grp'=4,'rep'=4,'sub'=2] {'rep'}, dimensions={0} | all-to-all | bytes 2097152 | tf_op jit(solution)/shard_map/all_to_all | solution.py:247
  376.5 19.1 %all_to_all.92 = bf16[8,256,256]{2,1,0:T(8,128)(2,1)} all-to-all(bf16[8,256,256]{2,1,0:T(8,128)(2,1)} %bitcast.217), channel_id=1, replica_groups=mesh['grp'=4,'rep'=4,'sub'=2] {'grp','sub'}, dimensions={0} | all-to-all | bytes 2097152 | tf_op jit(solution)/shard_map/all_to_all | solution.py:256
  414.1 30.0 %all-gather.20.cloned.1.call-done = bf16[2048,1024]{1,0:T(8,128)(2,1)} async-done(((bf16[512,1024]{1,0:T(8,128)(2,1)}), bf16[2048,1024]{1,0:T(8,128)(2,1)}) %all-gather.20.cloned.1.call-update) | async-done | bytes 4194320 | tf_op jit(solution)/shard_map/all_gather | solution.py:163
  449.0 53.0 %all-gather.16.cloned.1.call-done = bf16[2048,2048]{1,0:T(8,128)(2,1)} async-done(((bf16[256,2048]{1,0:T(8,128)(2,1)}), bf16[2048,2048]{1,0:T(8,128)(2,1)}) %all-gather.16.cloned.1.call-update) | async-done | bytes 8388624 | tf_op jit(solution)/shard_map/all_gather | solution.py:261
  502.0 14.4 fusion.70
  516.5 41.9 %all-gather.22.cloned.1.call-done = bf16[2048,2048]{1,0:T(8,128)(2,1)} async-done(((bf16[256,2048]{1,0:T(8,128)(2,1)}), bf16[2048,2048]{1,0:T(8,128)(2,1)}) %all-gather.22.cloned.1.call-update) | async-done | bytes 8388624 | tf_op jit(solution)/shard_map/all_gather | solution.py:262
  558.3 33.5 %convert_reduce_fusion = (f32[1024]{0:T(1024)}, bf16[2048,1024]{1,0:T(8,128)(2,1)S(1)}, f32[2048,1024]{1,0:T(8,128)}) fusion(f32[2048,1024]{1,0:T(8,128)} %fusion.70, f32[1024]{0:T(1024)S(1)} %dynamic_slice.42, bf16[2048,2048]{1,0:T(8,128)(2,1)} %all-gather.22.cloned.1.call-done, bf16[2048,1024]{1,0:T(8,128)(2,1)} %bitcast.207), kind=kOutput, calls=%fused_computation.46 | convolution fusion | flops 8747219968 | bytes 33562624 | tf_op jit(solution)/shard_map/dot_general | solution.py:54
  615.6 14.2 convolution_convert_fusion.3
  645.7 30.6 %reduce-scatter.10.cloned.1.call-done = bf16[256,2048]{1,0:T(8,128)(2,1)} async-done(((bf16[2048,2048]{1,0:T(8,128)(2,1)}), bf16[256,2048]{1,0:T(8,128)(2,1)}) %reduce-scatter.10.cloned.1.call-update) | async-done | bytes 1048592 | tf_op jit(solution)/shard_map/reduce_scatter | solution.py:271
  679.1 72.3 %reduce-scatter.8.cloned.1.call-done = bf16[256,2048]{1,0:T(8,128)(2,1)} async-done(((bf16[2048,2048]{1,0:T(8,128)(2,1)}), bf16[256,2048]{1,0:T(8,128)(2,1)}) %reduce-scatter.8.cloned.1.call-update) | async-done | bytes 1048592 | tf_op jit(solution)/shard_map/reduce_scatter | solution.py:275
  768.1 14.9 all-to-all-done.6
  813.6 26.1 %all-to-all-done.7 = bf16[4,512,256]{2,1,0:T(8,128)(2,1)S(1)} async-done(((bf16[4,512,256]{2,1,0:T(8,128)(2,1)}), bf16[4,512,256]{2,1,0:T(8,128)(2,1)S(1)}, u32[]{:S(2)}, u32[]{:S(2)}) %all-to-all-start.7) | async-done | bytes 1048608 | tf_op jit(solution)/shard_map/all_to_all | solution.py:290
  841.1 112.7 %while.28 = (s32[]{:T(128)}, f32[2048,2,128]{0,2,1:T(8,128)}, f32[2048,2,128]{0,2,1:T(8,128)}, bf16[4,512,2,128]{3,1,0,2:T(8,128)(2,1)}, s32[4]{0:T(128)S(1)}, /...) while((s32[]{:T(128)}, f32[2048,2,128]{0,2,1:T(8,128)}, ...), condition=%wide.region_15.16_spmd.clone, body=%wide.region_13.15_spmd.clone.sunk | while | flops 2721709056 | bytes 147901232 | solution.py:147
  968.3 73.6 %all_to_all.93 = bf16[4,512,768]{1,2,0:T(8,128)(2,1)S(1)} all-to-all(bf16[4,512,768]{1,2,0:T(8,128)(2,1)S(1)} %copy.180), channel_id=1, replica_groups=mesh['grp'=4,'rep'=4,'sub'=2] {'rep'}, dimensions={0} | all-to-all | bytes 6291456 | tf_op jit(solution)/shard_map/all_to_all | solution.py:247
  1079.3 14.8 all-to-all-done.10
  1126.2 17.7 %all-to-all-done.9 = bf16[8,64,768]{2,1,0:T(8,128)(2,1)} async-done(((bf16[8,64,768]{2,1,0:T(8,128)(2,1)}), bf16[8,64,768]{2,1,0:T(8,128)(2,1)}, u32[]{:S(2)}, u32[]{:S(2)}) %all-to-all-start.9) | async-done | bytes 786464 | tf_op jit(solution)/shard_map/all_to_all | solution.py:176
  1146.5 161.7 %reduce-scatter.16.cloned.1.call-done = bf16[64,2048]{1,0:T(8,128)(2,1)} async-done(((bf16[2048,2048]{1,0:T(8,128)(2,1)}), bf16[64,2048]{1,0:T(8,128)(2,1)}) %reduce-scatter.16.cloned.1.call-update) | async-done | bytes 262160 | tf_op jit(solution)/shard_map/reduce_scatter | solution.py:333
  1310.0 72.0 %reduce-scatter.12.cloned.1.call-done = bf16[256,2048]{1,0:T(8,128)(2,1)} async-done(((bf16[2048,2048]{1,0:T(8,128)(2,1)}), bf16[256,2048]{1,0:T(8,128)(2,1)}) %reduce-scatter.12.cloned.1.call-update) | async-done | bytes 1048592 | tf_op jit(solution)/shard_map/reduce_scatter | solution.py:304
  1388.0 129.6 %all-reduce.3.cloned.1.call-done = (f32[2048]{0:T(1024)}, f32[2048]{0:T(1024)}, f32[2048]{0:T(1024)}, f32[2048]{0:T(1024)}, f32[2048]{0:T(1024)}, /*index=5*/f32...) async-done(((f32[2048]{0:T(1024)}, f32[2048]{0:T(1024)}, f32[2048]{0:T(1024)}, f32[2048]{0:T(1024)}, f32[2048]{0:T(1024)}, /*index=5*/f32[2048]{0:T(1024)}, ...) | async-done | bytes 98320 | tf_op jit(solution)/shard_map/psum | solution.py:317
  (340 shorter events, 466.0 us)
Async XLA Ops:
  7.2 78.3 %all-gather.12.cloned.1.call-start = ((), (), s32[]{:S(2)}) async-start(), calls=%async_computation.20 | async-start | bytes 3932160 | tf_op jit(solution)/shard_map/all_gather | solution.py:163
  24.4 118.9 %all-gather.10.cloned.1.call-start = ((), (), s32[]{:S(2)}) async-start(), calls=%async_computation.19 | async-start | bytes 9437184 | tf_op jit(solution)/shard_map/all_gather | solution.py:224
  27.3 370.6 %all-gather.14.cloned.1.call-start = ((), (), s32[]{:S(2)}) async-start(), calls=%async_computation.21 | async-start | bytes 8650752 | tf_op jit(solution)/shard_map/all_gather | solution.py:220
  29.1 18.4 %all-to-all-start.4 = ((bf16[64,8,1024]{2,0,1:T(8,128)(2,1)}), bf16[64,8,1024]{2,0,1:T(8,128)(2,1)S(1)}, u32[]{:S(2)}, u32[]{:S(2)}) async-start(bf16[64,8,1024]{2,0,1:T(8,128)(2,1)} %bitcast.167), calls=%async_computation.4 | async-start | bytes 2097152 | tf_op jit(solution)/shard_map/all_to_all | solution.py:156
  47.5 111.7 %all-to-all-start.5 = ((bf16[64,8,1024]{2,0,1:T(8,128)(2,1)}), bf16[64,8,1024]{2,0,1:T(8,128)(2,1)S(1)}, u32[]{:S(2)}, u32[]{:S(2)}) async-start(bf16[64,8,1024]{2,0,1:T(8,128)(2,1)} %bitcast.214), calls=%async_computation.5 | async-start | bytes 2097152 | tf_op jit(solution)/shard_map/all_to_all | solution.py:156
  51.1 358.1 %all-gather.18.cloned.1.call-start = ((), (), s32[]{:S(2)}) async-start(), calls=%async_computation.23 | async-start | bytes 5242880 | tf_op jit(solution)/shard_map/all_gather | solution.py:163
  159.3 106.1 %all-to-all-start.1 = ((bf16[4,512,768]{1,2,0:T(8,128)(2,1)}), bf16[4,512,768]{1,2,0:T(8,128)(2,1)}, u32[]{:S(2)}, u32[]{:S(2)}) async-start(bf16[4,512,768]{1,2,0:T(8,128)(2,1)} %copy.159), calls=%async_computation.1 | async-start | bytes 6291456 | tf_op jit(solution)/shard_map/all_to_all | solution.py:236
  164.5 279.6 %all-gather.20.cloned.1.call-start = ((), (), s32[]{:S(2)}) async-start(), calls=%async_computation.24 | async-start | bytes 5242880 | tf_op jit(solution)/shard_map/all_gather | solution.py:163
  174.8 327.2 %all-gather.16.cloned.1.call-start = ((), (), s32[]{:S(2)}) async-start(), calls=%async_computation.22 | async-start | bytes 9437184 | tf_op jit(solution)/shard_map/all_gather | solution.py:261
  407.6 150.8 %all-gather.22.cloned.1.call-start = ((), (), s32[]{:S(2)}) async-start(), calls=%async_computation.26 | async-start | bytes 9437184 | tf_op jit(solution)/shard_map/all_gather | solution.py:262
  408.3 268.0 %reduce-scatter.10.cloned.1.call-start = ((), (), s32[]{:S(2)}) async-start(), calls=%async_computation.27 | async-start | bytes 9437184 | tf_op jit(solution)/shard_map/reduce_scatter | solution.py:271
  604.9 146.6 %reduce-scatter.8.cloned.1.call-start = ((), (), s32[]{:S(2)}) async-start(), calls=%async_computation.25 | async-start | bytes 9437184 | tf_op jit(solution)/shard_map/reduce_scatter | solution.py:275
  629.8 445.9 %reduce-scatter.18.cloned.1.call-start = ((), (), s32[]{:S(2)}) async-start(), calls=%async_computation.31 | async-start | bytes 5242880 | tf_op jit(solution)/shard_map/reduce_scatter | solution.py:175
  763.8 19.2 %all-to-all-start.6 = ((bf16[8,256,256]{2,1,0:T(8,128)(2,1)}), bf16[8,256,256]{2,1,0:T(8,128)(2,1)}, u32[]{:S(2)}, u32[]{:S(2)}) async-start(bf16[8,256,256]{2,1,0:T(8,128)(2,1)} %bitcast.165), calls=%async_computation.8 | async-start | bytes 2097152 | tf_op jit(solution)/shard_map/all_to_all | solution.py:283
  783.0 56.7 %all-to-all-start.7 = ((bf16[4,512,256]{2,1,0:T(8,128)(2,1)}), bf16[4,512,256]{2,1,0:T(8,128)(2,1)S(1)}, u32[]{:S(2)}, u32[]{:S(2)}) async-start(bf16[4,512,256]{2,1,0:T(8,128)(2,1)} %bitcast.41), calls=%async_computation.9 | async-start | bytes 2097152 | tf_op jit(solution)/shard_map/all_to_all | solution.py:290
  788.1 291.2 %reduce-scatter.20.cloned.1.call-start = ((), (), s32[]{:S(2)}) async-start(), calls=%async_computation.32 | async-start | bytes 5242880 | tf_op jit(solution)/shard_map/reduce_scatter | solution.py:175
  813.6 303.4 %reduce-scatter.14.cloned.1.call-start = ((), (), s32[]{:S(2)}) async-start(), calls=%async_computation.29 | async-start | bytes 3932160 | tf_op jit(solution)/shard_map/reduce_scatter | solution.py:175
  1057.4 250.7 %reduce-scatter.16.cloned.1.call-start = ((), (), s32[]{:S(2)}) async-start(), calls=%async_computation.30 | async-start | bytes 8650752 | tf_op jit(solution)/shard_map/reduce_scatter | solution.py:333
  1064.2 317.8 %reduce-scatter.12.cloned.1.call-start = ((), (), s32[]{:S(2)}) async-start(), calls=%async_computation.28 | async-start | bytes 9437184 | tf_op jit(solution)/shard_map/reduce_scatter | solution.py:304
  1075.7 18.4 %all-to-all-start.10 = ((bf16[8,64,1024]{2,1,0:T(8,128)(2,1)}), bf16[8,64,1024]{2,1,0:T(8,128)(2,1)S(1)}, u32[]{:S(2)}, u32[]{:S(2)}) async-start(bf16[8,64,1024]{2,1,0:T(8,128)(2,1)} %bitcast.236), calls=%async_computation.16 | async-start | bytes 2097152 | tf_op jit(solution)/shard_map/all_to_all | solution.py:176
  1095.1 18.4 %all-to-all-start.11 = ((bf16[8,64,1024]{2,1,0:T(8,128)(2,1)}), bf16[8,64,1024]{2,1,0:T(8,128)(2,1)S(1)}, u32[]{:S(2)}, u32[]{:S(2)}) async-start(bf16[8,64,1024]{2,1,0:T(8,128)(2,1)} %bitcast.237), calls=%async_computation.18 | async-start | bytes 2097152 | tf_op jit(solution)/shard_map/all_to_all | solution.py:176
  1116.9 27.0 %all-to-all-start.9 = ((bf16[8,64,768]{2,1,0:T(8,128)(2,1)}), bf16[8,64,768]{2,1,0:T(8,128)(2,1)}, u32[]{:S(2)}, u32[]{:S(2)}) async-start(bf16[8,64,768]{2,1,0:T(8,128)(2,1)} %bitcast.242), calls=%async_computation.13 | async-start | bytes 1572864 | tf_op jit(solution)/shard_map/all_to_all | solution.py:176
  1121.1 396.4 %all-reduce.3.cloned.1.call-start = ((), (), s32[]{:S(2)}) async-start(), calls=%async_computation.33 | async-start | bytes 196608 | tf_op jit(solution)/shard_map/psum | solution.py:317
  1122.9 259.1 %copy-start.39 = (f32[256]{0:T(256)S(1)}, f32[256]{0:T(256)}, u32[]{:S(2)}) copy-start(f32[256]{0:T(256)} %copy-done.38) | copy-start | bytes 3076
  (57 other events, 2373.5 us)
Sparse Core Ops, SparseCore 0:
  24.5 60.9 all-gather.11
  87.9 55.3 all-gather.9
  146.3 122.2 all-gather.13
  270.6 84.9 all-gather.17
  357.0 87.0 all-gather.19
  446.4 55.5 all-gather.15
  503.9 54.3 all-gather.21
  605.0 71.2 reduce-scatter.9
  680.2 71.2 reduce-scatter.7
  753.6 99.2 reduce-scatter.17
  855.3 75.8 reduce-scatter.19
  1057.6 59.3 reduce-scatter.13
  1119.2 188.9 reduce-scatter.15
  1311.5 70.4 reduce-scatter.11
  1390.6 126.9 all-reduce.2
where the time goes:
time: 1540 us
  waiting for transfers between devices  873 us (57%)
  matrix products  256 us (17%)
  blocking collectives  155 us (10%)
  local copies, waits for them, and re-layouts  124 us (8%)
  other arithmetic  72.8 us (5%)
  starting transfers between devices  34.3 us (2%)
    reduce_scatter x1, waiting for transfers between devices, shards(): lax.psum_scatter(row_outer(attended, branch_slope).astype(jnp.bfloat16),...  162 us
    psum x1, waiting for transfers between devices, shards(): lax.psum((jnp.sum(entry_slope * entry_normal, axis=0), jnp.sum(entry_slop...  130 us
    all_to_all x2, blocking collectives, to_tokens(): lax.all_to_all(array.reshape(reps, plane_rows // reps, columns), 'rep', s...  110 us
    all_to_all x1, waiting for transfers between devices, shards(): lax.all_to_all(joint_values.reshape(groups, plane_rows // groups, 3 * hea...  90 us
    reduce_scatter x1, waiting for transfers between devices, shards(): lax.psum_scatter(output_part, PLANE, scatter_dimension=0, tiled=True)  72.3 us
    reduce_scatter x1, waiting for transfers between devices, shards(): lax.psum_scatter(entry_part, PLANE, scatter_dimension=0, tiled=True)  72 us
    dot_general x4, matrix products, product(): jnp.dot(left_matrix, right_matrix, preferred_element_type=jnp.float32)  65.4 us
    all_gather x3, waiting for transfers between devices, plane_columns(): every = lax.all_gather(own, 'rep', axis=0, tiled=True)  63.8 us
  transfers between devices with their start and end apart: 23, of which 18 were waited for; matrix products, arithmetic and copies ran while one was open for 25% of the time, Pallas kernels for 0%

commit v1 on v0

--- a/solution.py
+++ b/solution.py
@@ -258,8 +258,13 @@
     residual = input_float + (product(attended, mixing_whole) + attention_offset)
     middle_normal, middle_inverse = norm_terms(residual)
     middle_normed = (middle_normal * middle_gain + middle_shift).astype(jnp.bfloat16)
-    middle_all = lax.all_gather(middle_normed, PLANE, axis=0, tiled=True)
-    cotangent_all = lax.all_gather(cotangent, PLANE, axis=0, tiled=True)
+    middle_all, cotangent_all = jnp.split(
+        lax.all_gather(
+            jnp.concatenate([middle_normed, cotangent], axis=1), PLANE, axis=0, tiled=True
+        ),
+        [middle_normed.shape[1]],
+        axis=1,
+    )
     hidden_local = hidden_width // plane_count
     offset_local = lax.dynamic_slice_in_dim(expand_offset, plane_index * hidden_local, hidden_local)
     expanded = product(middle_all, expand_slice) + offset_local

time: 1540 us -> 1540 us (level)
    all_gather x2 -> x1, waiting for transfers between devices: 94.9 us -> 88.4 us  [shards(): lax.all_gather(jnp.concatenate([middle_normed, cotangent], axis=1), PLANE...]
  transfers between devices with their start and end apart: 23 -> 22, of which waited for: 18 -> 17; matrix products, arithmetic and copies ran while one was open for 25% -> 23% of each run, Pallas kernels for 0% -> 0%
where the time goes in v1:
time: 1540 us; the launch traced here: 1530 us
  waiting for transfers between devices  887 us (58%)
  matrix products  262 us (17%)
  blocking collectives  156 us (10%)
  local copies, waits for them, and re-layouts  113 us (7%)
  other arithmetic  62.6 us (4%)
  starting transfers between devices  33.7 us (2%)
    reduce_scatter x1, waiting for transfers between devices, shards(): lax.psum_scatter(row_outer(attended, branch_slope).astype(jnp.bfloat16),...  160 us
    psum x1, waiting for transfers between devices, shards(): lax.psum((jnp.sum(entry_slope * entry_normal, axis=0), jnp.sum(entry_slop...  130 us
    all_to_all x2, blocking collectives, to_tokens(): lax.all_to_all(array.reshape(reps, plane_rows // reps, columns), 'rep', s...  110 us
    all_to_all x1, waiting for transfers between devices, shards(): lax.all_to_all(joint_values.reshape(groups, plane_rows // groups, 3 * hea...  90.4 us
    all_gather x1, waiting for transfers between devices, shards(): lax.all_gather(jnp.concatenate([middle_normed, cotangent], axis=1), PLANE...  88.4 us
    reduce_scatter x1, waiting for transfers between devices, shards(): lax.psum_scatter(entry_part, PLANE, scatter_dimension=0, tiled=True)  72.8 us
    reduce_scatter x1, waiting for transfers between devices, shards(): lax.psum_scatter(output_part, PLANE, scatter_dimension=0, tiled=True)  72.3 us
    dot_general x4, matrix products, product(): jnp.dot(left_matrix, right_matrix, preferred_element_type=jnp.float32)  70.2 us
  transfers between devices with their start and end apart: 22, of which 17 were waited for; matrix products, arithmetic and copies ran while one was open for 23% of the time, Pallas kernels for 0%

profile of v1, /device:TPU:8, one launch (start us, length us, event | category | flops | bytes accessed | tf_op | source)
XLA Modules:
  0.0 1534.6 jit_solution(5985623458741168601)
XLA Ops:
  8.5 15.8 %all_to_all.90 = bf16[64,8,768]{2,0,1:T(8,128)(2,1)} all-to-all(bf16[64,8,768]{2,0,1:T(8,128)(2,1)S(1)} %bitcast.221), channel_id=1, replica_groups=mesh['grp'=4,'rep'=4,'sub'=2] {'grp','sub'}, dimensions={1} | all-to-all | bytes 1572864 | tf_op jit(solution)/shard_map/all_to_all | solution.py:156
  34.0 13.5 all-to-all-done.4
  51.6 33.9 %all-gather.11.cloned.1.call-done = bf16[2048,768]{1,0:T(8,128)(2,1)} async-done(((bf16[512,768]{1,0:T(8,128)(2,1)}), bf16[2048,768]{1,0:T(8,128)(2,1)}) %all-gather.11.cloned.1.call-update) | async-done | bytes 3145744 | tf_op jit(solution)/shard_map/all_gather | solution.py:163
  89.4 54.0 %all-gather.9.cloned.1.call-done = bf16[2048,2048]{1,0:T(8,128)(2,1)} async-done(((bf16[256,2048]{1,0:T(8,128)(2,1)}), bf16[2048,2048]{1,0:T(8,128)(2,1)}) %all-gather.9.cloned.1.call-update) | async-done | bytes 8388624 | tf_op jit(solution)/shard_map/all_gather | solution.py:224
  175.0 90.4 %all-to-all-done.1 = bf16[4,512,768]{1,2,0:T(8,128)(2,1)} async-done(((bf16[4,512,768]{1,2,0:T(8,128)(2,1)}), bf16[4,512,768]{1,2,0:T(8,128)(2,1)}, u32[]{:S(2)}, u32[]{:S(2)}) %all-to-all-start.1) | async-done | bytes 3145760 | tf_op jit(solution)/shard_map/all_to_all | solution.py:236
  284.3 53.2 %while.27 = (s32[]{:T(128)}, bf16[4,512,2,128]{1,3,2,0:T(8,128)(2,1)}, f32[4,512,2]{1,2,0:T(2,128)}, s32[2048]{0:T(1024)S(1)}, s32[4]{0:T(128)S(1)}, /*index=5*/...) while((s32[]{:T(128)}, ...), condition=%wide.region_6.7_spmd, body=%wide.region_3.6_spmd.sunk | while | flops 1100086272 | bytes 33086656 | solution.py:96
  337.6 36.6 %all_to_all.91 = bf16[4,512,256]{1,2,0:T(8,128)(2,1)} all-to-all(bf16[4,512,256]{1,2,0:T(8,128)(2,1)} %bitcast.232), channel_id=1, replica_groups=mesh['grp'=4,'rep'=4,'sub'=2] {'rep'}, dimensions={0} | all-to-all | bytes 2097152 | tf_op jit(solution)/shard_map/all_to_all | solution.py:247
  376.5 19.3 %all_to_all.92 = bf16[8,256,256]{2,1,0:T(8,128)(2,1)} all-to-all(bf16[8,256,256]{2,1,0:T(8,128)(2,1)} %bitcast.211), channel_id=1, replica_groups=mesh['grp'=4,'rep'=4,'sub'=2] {'grp','sub'}, dimensions={0} | all-to-all | bytes 2097152 | tf_op jit(solution)/shard_map/all_to_all | solution.py:256
  414.0 30.1 %all-gather.19.cloned.1.call-done = bf16[2048,1024]{1,0:T(8,128)(2,1)} async-done(((bf16[512,1024]{1,0:T(8,128)(2,1)}), bf16[2048,1024]{1,0:T(8,128)(2,1)}) %all-gather.19.cloned.1.call-update) | async-done | bytes 4194320 | tf_op jit(solution)/shard_map/all_gather | solution.py:163
  449.0 88.4 %all-gather.15.cloned.1.call-done = bf16[2048,4096]{1,0:T(8,128)(2,1)} async-done(((bf16[256,4096]{1,0:T(8,128)(2,1)}), bf16[2048,4096]{1,0:T(8,128)(2,1)}) %all-gather.15.cloned.1.call-update) | async-done | bytes 16777232 | tf_op jit(solution)/shard_map/all_gather | solution.py:262
  537.5 31.8 %multiply_convert_fusion.1 = (bf16[2048,1024]{1,0:T(8,128)(2,1)}, f32[2048,1024]{1,0:T(8,128)}, f32[2048,1024]{1,0:T(8,128)}) fusion(f32[1024]{0:T(1024)S(1)} %dynamic_slice.42, bf16[2048,1024]{1,0:T(8,128)(2,1)} %bitcast.202, bf16[2048,4096]{1,0:T(8,128)(2,1)} %all-gather.15.cloned.1.call-done), kind=kOutput, calls=%fused_computation.48 | convolution fusion | flops 8728346624 | bytes 33558528 | tf_op jit(solution)/shard_map/dot_general | solution.py:54
  569.3 20.9 %convert_reduce_fusion = (f32[1024]{0:T(1024)}, bf16[2048,1024]{1,0:T(8,128)(2,1)}) fusion(f32[2048,1024]{1,0:T(8,128)} %get-tuple-element.340, bf16[2048,1024]{1,0:T(8,128)(2,1)S(1)} %bitcast.201, bf16[2048,4096]{1,0:T(8,128)(2,1)} %all-gather.15.cloned.1.call-done, f32[2048,1024]{1,0:T(8,128)} %get-tuple-element.354, f32[1024]{0:T(1024)S(1)} %dynamic_slice.42), kind=kOutput, calls=%fused_computation.46 | convolution fusion | flops 8625585152 | bytes 33562624 | tf_op jit(solution)/shard_map/dot_general | solution.py:54
  603.7 14.4 convolution_convert_fusion.3
  634.1 41.0 %reduce-scatter.10.cloned.1.call-done = bf16[256,2048]{1,0:T(8,128)(2,1)} async-done(((bf16[2048,2048]{1,0:T(8,128)(2,1)}), bf16[256,2048]{1,0:T(8,128)(2,1)}) %reduce-scatter.10.cloned.1.call-update) | async-done | bytes 1048592 | tf_op jit(solution)/shard_map/reduce_scatter | solution.py:276
  677.9 72.3 %reduce-scatter.8.cloned.1.call-done = bf16[256,2048]{1,0:T(8,128)(2,1)} async-done(((bf16[2048,2048]{1,0:T(8,128)(2,1)}), bf16[256,2048]{1,0:T(8,128)(2,1)}) %reduce-scatter.8.cloned.1.call-update) | async-done | bytes 1048592 | tf_op jit(solution)/shard_map/reduce_scatter | solution.py:280
  766.7 14.9 all-to-all-done.6
  802.5 35.6 %all-to-all-done.7 = bf16[4,512,256]{2,1,0:T(8,128)(2,1)S(1)} async-done(((bf16[4,512,256]{2,1,0:T(8,128)(2,1)}), bf16[4,512,256]{2,1,0:T(8,128)(2,1)S(1)}, u32[]{:S(2)}, u32[]{:S(2)}) %all-to-all-start.7) | async-done | bytes 1048608 | tf_op jit(solution)/shard_map/all_to_all | solution.py:295
  839.2 112.5 %while.28 = (s32[]{:T(128)}, f32[2048,2,128]{0,2,1:T(8,128)}, f32[2048,2,128]{0,2,1:T(8,128)}, bf16[4,512,2,128]{3,1,0,2:T(8,128)(2,1)}, s32[4]{0:T(128)S(1)}, /...) while((s32[]{:T(128)}, f32[2048,2,128]{0,2,1:T(8,128)}, ...), condition=%wide.region_15.16_spmd.clone, body=%wide.region_13.15_spmd.clone.sunk | while | flops 2721709056 | bytes 147901232 | solution.py:147
  966.3 73.8 %all_to_all.93 = bf16[4,512,768]{1,2,0:T(8,128)(2,1)S(1)} all-to-all(bf16[4,512,768]{1,2,0:T(8,128)(2,1)S(1)} %copy.176), channel_id=1, replica_groups=mesh['grp'=4,'rep'=4,'sub'=2] {'rep'}, dimensions={0} | all-to-all | bytes 6291456 | tf_op jit(solution)/shard_map/all_to_all | solution.py:247
  1077.4 14.8 all-to-all-done.10
  1124.4 18.6 %all-to-all-done.9 = bf16[8,64,768]{2,1,0:T(8,128)(2,1)} async-done(((bf16[8,64,768]{2,1,0:T(8,128)(2,1)}), bf16[8,64,768]{2,1,0:T(8,128)(2,1)}, u32[]{:S(2)}, u32[]{:S(2)}) %all-to-all-start.9) | async-done | bytes 786464 | tf_op jit(solution)/shard_map/all_to_all | solution.py:176
  1145.6 160.4 %reduce-scatter.16.cloned.1.call-done = bf16[64,2048]{1,0:T(8,128)(2,1)} async-done(((bf16[2048,2048]{1,0:T(8,128)(2,1)}), bf16[64,2048]{1,0:T(8,128)(2,1)}) %reduce-scatter.16.cloned.1.call-update) | async-done | bytes 262160 | tf_op jit(solution)/shard_map/reduce_scatter | solution.py:338
  1307.8 72.8 %reduce-scatter.12.cloned.1.call-done = bf16[256,2048]{1,0:T(8,128)(2,1)} async-done(((bf16[2048,2048]{1,0:T(8,128)(2,1)}), bf16[256,2048]{1,0:T(8,128)(2,1)}) %reduce-scatter.12.cloned.1.call-update) | async-done | bytes 1048592 | tf_op jit(solution)/shard_map/reduce_scatter | solution.py:309
  1386.6 129.6 %all-reduce.3.cloned.1.call-done = (f32[2048]{0:T(1024)}, f32[2048]{0:T(1024)}, f32[2048]{0:T(1024)}, f32[2048]{0:T(1024)}, f32[2048]{0:T(1024)}, /*index=5*/f32...) async-done(((f32[2048]{0:T(1024)}, f32[2048]{0:T(1024)}, f32[2048]{0:T(1024)}, f32[2048]{0:T(1024)}, f32[2048]{0:T(1024)}, /*index=5*/f32[2048]{0:T(1024)}, ...) | async-done | bytes 98320 | tf_op jit(solution)/shard_map/psum | solution.py:322
  (336 shorter events, 431.3 us)
Async XLA Ops:
  7.2 78.3 %all-gather.11.cloned.1.call-start = ((), (), s32[]{:S(2)}) async-start(), calls=%async_computation.20 | async-start | bytes 3932160 | tf_op jit(solution)/shard_map/all_gather | solution.py:163
  24.4 118.9 %all-gather.9.cloned.1.call-start = ((), (), s32[]{:S(2)}) async-start(), calls=%async_computation.19 | async-start | bytes 9437184 | tf_op jit(solution)/shard_map/all_gather | solution.py:224
  27.2 370.8 %all-gather.13.cloned.1.call-start = ((), (), s32[]{:S(2)}) async-start(), calls=%async_computation.21 | async-start | bytes 8650752 | tf_op jit(solution)/shard_map/all_gather | solution.py:220
  29.1 18.4 %all-to-all-start.4 = ((bf16[64,8,1024]{2,0,1:T(8,128)(2,1)}), bf16[64,8,1024]{2,0,1:T(8,128)(2,1)S(1)}, u32[]{:S(2)}, u32[]{:S(2)}) async-start(bf16[64,8,1024]{2,0,1:T(8,128)(2,1)} %bitcast.161), calls=%async_computation.4 | async-start | bytes 2097152 | tf_op jit(solution)/shard_map/all_to_all | solution.py:156
  47.5 111.8 %all-to-all-start.5 = ((bf16[64,8,1024]{2,0,1:T(8,128)(2,1)}), bf16[64,8,1024]{2,0,1:T(8,128)(2,1)S(1)}, u32[]{:S(2)}, u32[]{:S(2)}) async-start(bf16[64,8,1024]{2,0,1:T(8,128)(2,1)} %bitcast.208), calls=%async_computation.5 | async-start | bytes 2097152 | tf_op jit(solution)/shard_map/all_to_all | solution.py:156
  51.1 358.0 %all-gather.17.cloned.1.call-start = ((), (), s32[]{:S(2)}) async-start(), calls=%async_computation.23 | async-start | bytes 5242880 | tf_op jit(solution)/shard_map/all_gather | solution.py:163
  159.3 106.1 %all-to-all-start.1 = ((bf16[4,512,768]{1,2,0:T(8,128)(2,1)}), bf16[4,512,768]{1,2,0:T(8,128)(2,1)}, u32[]{:S(2)}, u32[]{:S(2)}) async-start(bf16[4,512,768]{1,2,0:T(8,128)(2,1)} %copy.155), calls=%async_computation.1 | async-start | bytes 6291456 | tf_op jit(solution)/shard_map/all_to_all | solution.py:236
  164.4 279.6 %all-gather.19.cloned.1.call-start = ((), (), s32[]{:S(2)}) async-start(), calls=%async_computation.24 | async-start | bytes 5242880 | tf_op jit(solution)/shard_map/all_gather | solution.py:163
  174.8 362.6 %all-gather.15.cloned.1.call-start = ((), (), s32[]{:S(2)}) async-start(), calls=%async_computation.22 | async-start | bytes 18874368 | tf_op jit(solution)/shard_map/all_gather | solution.py:262
  408.3 266.8 %reduce-scatter.10.cloned.1.call-start = ((), (), s32[]{:S(2)}) async-start(), calls=%async_computation.26 | async-start | bytes 9437184 | tf_op jit(solution)/shard_map/reduce_scatter | solution.py:276
  603.7 146.6 %reduce-scatter.8.cloned.1.call-start = ((), (), s32[]{:S(2)}) async-start(), calls=%async_computation.25 | async-start | bytes 9437184 | tf_op jit(solution)/shard_map/reduce_scatter | solution.py:280
  618.1 455.7 %reduce-scatter.18.cloned.1.call-start = ((), (), s32[]{:S(2)}) async-start(), calls=%async_computation.30 | async-start | bytes 5242880 | tf_op jit(solution)/shard_map/reduce_scatter | solution.py:175
  762.4 19.2 %all-to-all-start.6 = ((bf16[8,256,256]{2,1,0:T(8,128)(2,1)}), bf16[8,256,256]{2,1,0:T(8,128)(2,1)}, u32[]{:S(2)}, u32[]{:S(2)}) async-start(bf16[8,256,256]{2,1,0:T(8,128)(2,1)} %bitcast.159), calls=%async_computation.8 | async-start | bytes 2097152 | tf_op jit(solution)/shard_map/all_to_all | solution.py:288
  781.6 56.5 %all-to-all-start.7 = ((bf16[4,512,256]{2,1,0:T(8,128)(2,1)}), bf16[4,512,256]{2,1,0:T(8,128)(2,1)S(1)}, u32[]{:S(2)}, u32[]{:S(2)}) async-start(bf16[4,512,256]{2,1,0:T(8,128)(2,1)} %bitcast.41), calls=%async_computation.9 | async-start | bytes 2097152 | tf_op jit(solution)/shard_map/all_to_all | solution.py:295
  786.8 290.7 %reduce-scatter.20.cloned.1.call-start = ((), (), s32[]{:S(2)}) async-start(), calls=%async_computation.31 | async-start | bytes 5242880 | tf_op jit(solution)/shard_map/reduce_scatter | solution.py:175
  802.4 312.7 %reduce-scatter.14.cloned.1.call-start = ((), (), s32[]{:S(2)}) async-start(), calls=%async_computation.28 | async-start | bytes 3932160 | tf_op jit(solution)/shard_map/reduce_scatter | solution.py:175
  1055.6 250.5 %reduce-scatter.16.cloned.1.call-start = ((), (), s32[]{:S(2)}) async-start(), calls=%async_computation.29 | async-start | bytes 8650752 | tf_op jit(solution)/shard_map/reduce_scatter | solution.py:338
  1062.3 318.3 %reduce-scatter.12.cloned.1.call-start = ((), (), s32[]{:S(2)}) async-start(), calls=%async_computation.27 | async-start | bytes 9437184 | tf_op jit(solution)/shard_map/reduce_scatter | solution.py:309
  1073.8 18.4 %all-to-all-start.10 = ((bf16[8,64,1024]{2,1,0:T(8,128)(2,1)}), bf16[8,64,1024]{2,1,0:T(8,128)(2,1)S(1)}, u32[]{:S(2)}, u32[]{:S(2)}) async-start(bf16[8,64,1024]{2,1,0:T(8,128)(2,1)} %bitcast.230), calls=%async_computation.16 | async-start | bytes 2097152 | tf_op jit(solution)/shard_map/all_to_all | solution.py:176
  1093.2 18.4 %all-to-all-start.11 = ((bf16[8,64,1024]{2,1,0:T(8,128)(2,1)}), bf16[8,64,1024]{2,1,0:T(8,128)(2,1)S(1)}, u32[]{:S(2)}, u32[]{:S(2)}) async-start(bf16[8,64,1024]{2,1,0:T(8,128)(2,1)} %bitcast.231), calls=%async_computation.18 | async-start | bytes 2097152 | tf_op jit(solution)/shard_map/all_to_all | solution.py:176
  1115.2 27.8 %all-to-all-start.9 = ((bf16[8,64,768]{2,1,0:T(8,128)(2,1)}), bf16[8,64,768]{2,1,0:T(8,128)(2,1)}, u32[]{:S(2)}, u32[]{:S(2)}) async-start(bf16[8,64,768]{2,1,0:T(8,128)(2,1)} %bitcast.236), calls=%async_computation.13 | async-start | bytes 1572864 | tf_op jit(solution)/shard_map/all_to_all | solution.py:176
  1119.4 396.7 %all-reduce.3.cloned.1.call-start = ((), (), s32[]{:S(2)}) async-start(), calls=%async_computation.32 | async-start | bytes 196608 | tf_op jit(solution)/shard_map/psum | solution.py:322
  1121.2 259.4 %copy-start.36 = (f32[256]{0:T(256)S(1)}, f32[256]{0:T(256)}, u32[]{:S(2)}) copy-start(f32[256]{0:T(256)} %copy-done.35) | copy-start | bytes 3076
  1121.2 259.4 %copy-start.40 = (f32[256]{0:T(256)S(1)}, f32[256]{0:T(256)}, u32[]{:S(2)}) copy-start(f32[256]{0:T(256)} %copy-done.39) | copy-start | bytes 3076
  (56 other events, 2222.3 us)
Sparse Core Ops, SparseCore 0:
  24.5 60.9 all-gather.10
  87.9 55.3 all-gather.8
  146.3 122.2 all-gather.12
  270.6 84.8 all-gather.16
  357.0 87.0 all-gather.18
  446.4 91.0 all-gather.14
  603.8 71.2 reduce-scatter.9
  678.9 71.2 reduce-scatter.7
  752.5 99.2 reduce-scatter.17
  854.0 75.8 reduce-scatter.19
  1055.7 59.4 reduce-scatter.13
  1117.3 188.6 reduce-scatter.15
  1309.5 71.0 reduce-scatter.11
  1389.1 126.9 all-reduce.2
